TPU v7x, 32 devices: a whole 2x2x4 slice. The times are simulated.
32 devices in a mesh: elem: 8 (over z, y), bucket: 4 (over x, core).
Axes of the slice: x: 2, y: 2, z: 4, core: 2. Of those that a mesh axis runs over, the one named last changes fastest.
Arguments:
- node_data: float32 [24, 98304], P(None, 'elem'), may hold values from -6 to 6
- eroded: int32 [4096], P('elem'), may hold values from 0 to 2047, as said below
- bucket_map: int32 [98304], P('elem'), may hold values from 0 to 63, as said below
- seg_point: float32 [64, 3, 512], P('elem', None, 'bucket'), may hold values from -3 to 3
- seg_angle: float32 [64, 2, 512], P('elem', None, 'bucket'), may hold values from -3.140625 to 3.140625
Outputs:
- face_force: float32 [3, 24576], P(None, 'elem')
Inputs may be any that keep to these rules, and one draw needn't show every extreme that they name: `eroded`: the 512 entries of one index of elem are distinct local element numbers. `bucket_map`: among the faces of the elements listed in eroded, those of one index of elem name one bucket at most 80 times; in every draw some bucket is named exactly 80 times by every index of elem.
All inputs are finite; a program needn't handle non-finite values.
Results may differ from a plain program's by a relative error of at most 0.00012.
Values sent between devices are 32-bit elements; how exact they have to be, the bound alone decides.
A program may use at most 64 MiB of HBM per device.

v0:
```python
import functools

import jax
import jax.numpy as jnp
from jax import lax
from jax.experimental import pallas as pl
from jax.experimental.pallas import tpu as pltpu
from jax.sharding import PartitionSpec as P

STIFFNESS = 20.0
DAMPING = 0.5
LANES = 128
SIDES = 6
BLOCK = SIDES * LANES
F32 = jnp.float32
BF16 = jnp.bfloat16


def split3(x):
    hi = x.astype(BF16).astype(F32)
    rest = x - hi
    mid = rest.astype(BF16).astype(F32)
    return hi, mid, rest - mid


def sin_cos(x):
    k = jnp.floor(x * 0.6366197723675814 + 0.5)
    r = x - k * 1.5703125
    r = r - k * 4.837512969970703125e-4
    r = r - k * 7.54978995489188216e-8
    z = r * r
    s = ((-1.9515295891e-4 * z + 8.3321608736e-3) * z - 1.6666654611e-1) * z * r + r
    c = ((2.443315711809948e-5 * z - 1.388731625493765e-3) * z + 4.166664568298827e-2) * z * z
    c = c - 0.5 * z + 1.0
    q = k.astype(jnp.int32) & 3
    odd = (q & 1) == 1
    sin = jnp.where(odd, c, s)
    cos = jnp.where(odd, s, c)
    sin = jnp.where(q >= 2, -sin, sin)
    cos = jnp.where((q == 1) | (q == 2), -cos, cos)
    return sin, cos


def mm(a, b, contract=((1,), (0,))):
    return lax.dot_general(a, b, (contract, ((), ())), preferred_element_type=F32)


def kernel(
    n_elem, n_buck, node_any, eroded, bmap, spoint, sangle, out,
    node, perm, pick, rows, faces, onehot, points, angles, values, seg_t, counts,
    sel0, sel1, sums_f, parts, inter,
    node_sem, seg_send, seg_recv, cnt_send, cnt_recv, par_send, par_recv,
):
    me = lax.axis_index("elem")
    mb = lax.axis_index("bucket")
    own = sangle.shape[0]
    buckets = own * n_elem
    count = eroded.shape[1]
    jblocks = count // LANES
    blocks = node.shape[1] // BLOCK
    chunks = parts.shape[1]
    mesh_ids = pl.DeviceIdType.MESH

    barrier = pltpu.get_barrier_semaphore()
    for d in range(1, n_elem):
        to = {"elem": lax.rem(me + d, n_elem)}
        pl.semaphore_signal(barrier, inc=1, device_id=to, device_id_type=mesh_ids)
    for d in range(1, n_buck):
        to = {"bucket": lax.rem(mb + d, n_buck)}
        pl.semaphore_signal(barrier, inc=1, device_id=to, device_id_type=mesh_ids)
    fetch = pltpu.make_async_copy(node_any, node, node_sem)
    fetch.start()

    col = lax.broadcasted_iota(jnp.int32, (1, BLOCK), 1)
    source = SIDES * (col & (LANES - 1)) + (col // LANES)
    for i in range(BLOCK // 256):
        r = lax.broadcasted_iota(jnp.int32, (256, BLOCK), 0) + i * 256
        perm[i * 256:(i + 1) * 256, :] = jnp.where(r == source, 1.0, 0.0).astype(BF16)
    for i in range(pick.shape[0] // 256):
        r = lax.broadcasted_iota(jnp.int32, (256, count), 0) + i * 256
        pick[i * 256:(i + 1) * 256, :] = jnp.where(r == eroded[...], 1.0, 0.0).astype(BF16)

    pl.semaphore_wait(barrier, n_elem + n_buck - 2)

    def seg_copies(slot, owner, target):
        at = pl.ds(pl.multiple_of(owner * own, own), own)
        return [
            pltpu.make_async_remote_copy(
                src_ref=src, dst_ref=dst,
                send_sem=seg_send.at[i, slot], recv_sem=seg_recv.at[i, slot],
                device_id={"elem": target}, device_id_type=mesh_ids,
            )
            for i, (src, dst) in enumerate(
                [(spoint, points.at[:, at]), (sangle, angles.at[at])]
            )
        ]

    for d in range(1, n_elem):
        for c in seg_copies(d - 1, me, lax.rem(me + d, n_elem)):
            c.start()

    fetch.wait()
    group = 4
    for g in range(blocks // group):
        stack = []
        for i in range(g * group, (g + 1) * group):
            lanes = slice(i * BLOCK, (i + 1) * BLOCK)
            c = [node[3 * v:3 * v + 3, lanes] for v in range(8)]
            e1, e2 = c[2] - c[0], c[3] - c[1]
            r1 = jnp.concatenate([e1[1:3], e1[0:1]], axis=0)
            r2 = jnp.concatenate([e2[1:3], e2[0:1]], axis=0)
            area = 0.5 * (e1 * r2 - r1 * e2)
            centroid = 0.25 * (((c[0] + c[1]) + c[2]) + c[3])
            velocity = 0.25 * (((c[4] + c[5]) + c[6]) + c[7])
            ids = bmap[:, lanes].astype(F32)
            two = jnp.zeros((2, BLOCK), F32)
            four = jnp.zeros((4, BLOCK), F32)
            first = jnp.concatenate([centroid, area, two], axis=0)
            second = jnp.concatenate([velocity, ids, four], axis=0)
            a, b = split3(first), split3(second)
            stack += [a[0], b[0], a[1], b[1], a[2]]
        apart = mm(jnp.concatenate(stack, axis=0).astype(BF16), perm[...]).astype(BF16)
        for i in range(group):
            at = (g * group + i) * LANES
            for s in range(SIDES):
                rows[s * 40:(s + 1) * 40, at:at + LANES] = apart[
                    i * 40:(i + 1) * 40, s * LANES:(s + 1) * LANES
                ]

    taken = mm(rows[...], pick[...])
    for s in range(SIDES):
        t = [taken[s * 40 + i * 8:s * 40 + i * 8 + 8] for i in range(5)]
        faces[s, 0:8, :] = (t[0] + t[2]) + t[4]
        faces[s, 8:16, :] = t[1] + t[3]

    ones = jnp.ones((8, count), BF16)
    chunk = min(buckets, LANES)
    for b in range(0, buckets, chunk):
        iota = lax.broadcasted_iota(jnp.int32, (chunk, count), 0) + b
        total = jnp.zeros((chunk, count), F32)
        for s in range(SIDES):
            ids = faces[s, 11:12, :].astype(jnp.int32)
            hot = jnp.where(iota == ids, 1.0, 0.0)
            total = total + hot
            onehot[b:b + chunk, s * count:(s + 1) * count] = hot.astype(BF16)
        if chunk < LANES:
            total = jnp.concatenate([total, jnp.zeros((LANES - chunk, count), F32)], axis=0)
        counts[me, :, b:b + LANES] = mm(ones, total.astype(BF16), ((1,), (1,)))

    def cnt_copy(slot, owner, target):
        return pltpu.make_async_remote_copy(
            src_ref=counts.at[owner], dst_ref=counts.at[owner],
            send_sem=cnt_send.at[slot], recv_sem=cnt_recv.at[slot],
            device_id={"elem": target}, device_id_type=mesh_ids,
        )

    for d in range(1, n_elem):
        cnt_copy(d - 1, me, lax.rem(me + d, n_elem)).start()

    def unfold(owner, p, a):
        at = pl.ds(pl.multiple_of(owner * own, own), own)
        sin0, cos0 = sin_cos(a[:, 0, :])
        sin1, cos1 = sin_cos(a[:, 1, :])
        for i, v in enumerate([p[0], p[1], p[2], cos0 * sin1, sin0 * sin1, cos1]):
            values[i, at, :] = v

    unfold(me, spoint[...], sangle[...])
    order = sorted(range(1, n_elem), key=lambda d: min(d, n_elem - d))
    for d in order:
        owner = lax.rem(me + n_elem - d, n_elem)
        for cp in seg_copies(d - 1, owner, me):
            cp.wait_recv()
        at = pl.ds(pl.multiple_of(owner * own, own), own)
        unfold(owner, points[:, at, :], angles[at])

    chunk = min(buckets, LANES // 2)

    def lay_out(b):
        for i in range(6):
            v = values[i, pl.ds(pl.multiple_of(b * chunk, chunk), chunk), :]
            stack = jnp.concatenate(list(split3(v)) + [jnp.zeros_like(v)], axis=0)
            lanes = pl.ds(pl.multiple_of(b * 4 * chunk, LANES), 4 * chunk)
            seg_t[i * LANES:(i + 1) * LANES, lanes] = stack.T.astype(BF16)

    if buckets == chunk:
        lay_out(0)
    else:
        pl.loop(0, buckets // chunk)(lay_out)

    for d in range(1, n_elem):
        cnt_copy(d - 1, lax.rem(me + n_elem - d, n_elem), me).wait_recv()
    whole = counts[0]
    for i in range(1, n_elem):
        whole = whole + counts[i]
    stiff = STIFFNESS * lax.rsqrt(jnp.maximum(whole[:, :buckets], 1.0))
    hi, mid, lo = split3(stiff)
    which = lax.broadcasted_iota(jnp.int32, stiff.shape, 0)
    stiff = jnp.where(which == 0, hi, jnp.where(which == 1, mid, jnp.where(which == 2, lo, 0.0)))
    stiff = mm(stiff.astype(BF16), onehot[...])
    stiff = (stiff[0:1] + stiff[1:2]) + stiff[2:3]
    for s in range(SIDES):
        faces[s, 12:13, :] = stiff[:, s * count:(s + 1) * count]

    half = 256
    halves = count // half
    steps = SIDES * halves

    def select(it, sel):
        hot = onehot[:, pl.ds(pl.multiple_of(it * half, half), half)]
        hot = [hot[b:b + chunk] for b in range(0, buckets, chunk) for _ in range(4)]
        sel[...] = mm(seg_t[...], jnp.concatenate(hot, axis=0))

    def forces(it, sel):
        s = it // halves
        h = it % halves
        for lt in range(half // LANES):
            g = faces[s, :, pl.ds(pl.multiple_of(h * half + lt * LANES, LANES), LANES)]
            cx, cy, cz, az, ax, ay, _, _, vx, vy, vz, _, stf = [
                jnp.broadcast_to(g[i:i + 1], (8, LANES)) for i in range(13)
            ]
            vx, vy, vz = DAMPING * vx, DAMPING * vy, DAMPING * vz
            acc = [jnp.zeros((8, LANES), F32) for _ in range(3)]
            for r in range(LANES // 8):
                px, py, pz, nx, ny, nz = [
                    sel[q * LANES + r * 8:q * LANES + r * 8 + 8, lt * LANES:(lt + 1) * LANES]
                    for q in range(6)
                ]
                ox, oy, oz = px - cx, py - cy, pz - cz
                dist = ox * ox + oy * oy + oz * oz
                depth = jnp.maximum(ox * nx + oy * ny + oz * nz, 0.0)
                proj = jnp.abs(ax * nx + ay * ny + az * nz)
                push = stf - (vx * nx + vy * ny + vz * nz)
                traction = (jnp.exp(-0.5 * dist) * depth) * (push * proj)
                for k, n in enumerate((nx, ny, nz)):
                    acc[k] = acc[k] + traction * n
            for k in range(3):
                at = it * (half // LANES) + lt
                sums_f[at, k:k + 1, :] = jnp.sum(acc[k], axis=0, keepdims=True)

    def par_copy(c, slot, owner, target):
        return pltpu.make_async_remote_copy(
            src_ref=parts.at[owner, c], dst_ref=parts.at[owner, c],
            send_sem=par_send.at[c, slot], recv_sem=par_recv.at[c, slot],
            device_id={"bucket": target}, device_id_type=mesh_ids,
        )

    wide = SIDES // chunks
    select(0, sel0)
    for c in range(chunks):
        base = c * steps // chunks

        def step(i, carry):
            it = base + 2 * i
            select(it + 1, sel1)
            forces(it, sel0)
            select(lax.rem(it + 2, steps), sel0)
            forces(it + 1, sel1)
            return carry

        lax.fori_loop(0, steps // chunks // 2, step, 0)
        for s in range(wide):
            for j in range(jblocks):
                f = sums_f[(c * wide + s) * jblocks + j]
                for k in range(3):
                    parts[mb, c, k, j:j + 1, s * LANES:(s + 1) * LANES] = f[k:k + 1]
        for d in range(1, n_buck):
            par_copy(c, d - 1, mb, lax.rem(mb + d, n_buck)).start()

    for c in range(chunks):
        for d in range(1, n_buck):
            par_copy(c, d - 1, lax.rem(mb + n_buck - d, n_buck), mb).wait_recv()
        for k in range(3):
            force = parts[0, c, k]
            for i in range(1, n_buck):
                force = force + parts[i, c, k]
            for p, v in enumerate(split3(force)):
                at = (p * 3 + k) * jblocks
                inter[at:at + jblocks, c * wide * LANES:(c + 1) * wide * LANES] = v
    used = 9 * jblocks
    if inter.shape[0] > used:
        inter[used:, :] = jnp.zeros((inter.shape[0] - used, BLOCK), F32)
    mixed = mm(inter[...].astype(BF16), perm[...], ((1,), (1,)))
    third = 3 * jblocks
    mixed = (mixed[0:third] + mixed[third:2 * third]) + mixed[2 * third:3 * third]
    for k in range(3):
        for j in range(jblocks):
            out[k:k + 1, j * BLOCK:(j + 1) * BLOCK] = mixed[k * jblocks + j:k * jblocks + j + 1]

    for d in range(1, n_elem):
        for cp in seg_copies(d - 1, me, lax.rem(me + d, n_elem)):
            cp.wait_send()
        cnt_copy(d - 1, me, lax.rem(me + d, n_elem)).wait_send()
    for c in range(chunks):
        for d in range(1, n_buck):
            par_copy(c, d - 1, mb, lax.rem(mb + d, n_buck)).wait_send()


def local(n_elem, n_buck, node_data, eroded, bucket_map, seg_point, seg_angle):
    own, _, segs = seg_point.shape
    buckets = own * n_elem
    count = eroded.shape[0]
    jblocks = count // LANES
    elems = node_data.shape[1] // SIDES
    pad = -(-9 * jblocks // 16) * 16
    vmem = pl.BlockSpec(memory_space=pltpu.VMEM)
    dma = pltpu.SemaphoreType.DMA
    return pl.pallas_call(
        functools.partial(kernel, n_elem, n_buck),
        out_shape=jax.ShapeDtypeStruct((3, SIDES * count), F32),
        in_specs=[pl.BlockSpec(memory_space=pl.ANY)] + [vmem] * 4,
        out_specs=vmem,
        scratch_shapes=[
            pltpu.VMEM(node_data.shape, F32),
            pltpu.VMEM((BLOCK, BLOCK), BF16),
            pltpu.VMEM((elems, count), BF16),
            pltpu.VMEM((SIDES * 40, elems), BF16),
            pltpu.VMEM((SIDES, 16, count), F32),
            pltpu.VMEM((buckets, SIDES * count), BF16),
            pltpu.VMEM((3, buckets, segs), F32),
            pltpu.VMEM((buckets, 2, segs), F32),
            pltpu.VMEM((6, buckets, segs), F32),
            pltpu.VMEM((6 * segs, 4 * buckets), BF16),
            pltpu.VMEM((n_elem, 8, max(buckets, LANES)), F32),
            pltpu.VMEM((6 * segs, 256), F32),
            pltpu.VMEM((6 * segs, 256), F32),
            pltpu.VMEM((SIDES * jblocks, 8, LANES), F32),
            pltpu.VMEM((n_buck, 3, 3, jblocks, BLOCK // 3), F32),
            pltpu.VMEM((pad, BLOCK), F32),
            dma,
            dma((2, n_elem - 1)),
            dma((2, n_elem - 1)),
            dma((n_elem - 1,)),
            dma((n_elem - 1,)),
            dma((3, n_buck - 1)),
            dma((3, n_buck - 1)),
        ],
        compiler_params=pltpu.CompilerParams(
            collective_id=0, has_side_effects=True, vmem_limit_bytes=60 * 1024 * 1024
        ),
        name="contact",
    )(node_data, eroded[None, :], bucket_map[None, :], seg_point.transpose(1, 0, 2), seg_angle)


def solution(mesh):
    in_specs = (
        P(None, "elem"),
        P("elem"),
        P("elem"),
        P("elem", None, "bucket"),
        P("elem", None, "bucket"),
    )
    body = functools.partial(local, mesh.shape["elem"], mesh.shape["bucket"])
    return jax.shard_map(
        body, mesh=mesh, in_specs=in_specs, out_specs=P(None, "elem"), check_vma=False
    )
```

profile of v0, /device:TPU:0, one launch (start us, length us, event | category | flops | bytes accessed | tf_op | source)
XLA Modules:
  0.0 21.7 jit_solution(7666908230957560125)
XLA Ops:
  0.0 20.2 %contact.1 = f32[3,3072]{1,0:T(4,128)} custom-call(f32[24,12288]{1,0:T(8,128)} %node_any.1, s32[1,512]{1,0:T(1,128)} %bitcast.5, s32[1,12288]{1,0:T(1,128)} %bitcast.3, f32[3,8,128]{2,1,0:T(8,128)} %bitcast.4, f32[8,2,128]{2,1,0:T(2,128)} %sangle.1), custom_call_target="tpu_custom_call" | custom-call | tf_op jit(solution)/shard_map/contact/pallas_call | solution.py:307
  20.2 1.4 %copy.7 = f32[3,3072]{1,0:T(4,128)} copy(f32[3,3072]{1,0:T(4,128)} %contact.1) | data formatting | bytes 73728
where the time goes:
time: 21.9 us; the launch traced here: 21.7 us
  Pallas kernels  20.2 us (92%)
  local copies, waits for them, and re-layouts  1.43 us (7%)
    pallas_call x1, Pallas kernels, local(): pl.pallas_call(functools.partial(kernel, n_elem, n_buck), out_shape=jax.S...  20.2 us
    unnamed x1, local copies, waits for them, and re-layouts  1.43 us

commit v1 on v0

v1 whole, which is shorter than its diff:
```python
import functools
import math

import jax
import jax.numpy as jnp
from jax import lax
from jax.experimental import pallas as pl
from jax.experimental.pallas import tpu as pltpu
from jax.sharding import PartitionSpec as P

STIFFNESS = 20.0
DAMPING = 0.5
SCALE = math.sqrt(0.5 / math.log(2.0))
LANES = 128
SIDES = 6
BLOCK = SIDES * LANES
F32 = jnp.float32
BF16 = jnp.bfloat16


def split3(x):
    hi = x.astype(BF16).astype(F32)
    rest = x - hi
    mid = rest.astype(BF16).astype(F32)
    return hi, mid, rest - mid


def sin_cos(x):
    k = jnp.floor(x * 0.6366197723675814 + 0.5)
    r = x - k * 1.5703125
    r = r - k * 4.837512969970703125e-4
    r = r - k * 7.54978995489188216e-8
    z = r * r
    s = ((-1.9515295891e-4 * z + 8.3321608736e-3) * z - 1.6666654611e-1) * z * r + r
    c = ((2.443315711809948e-5 * z - 1.388731625493765e-3) * z + 4.166664568298827e-2) * z * z
    c = c - 0.5 * z + 1.0
    q = k.astype(jnp.int32) & 3
    odd = (q & 1) == 1
    sin = jnp.where(odd, c, s)
    cos = jnp.where(odd, s, c)
    sin = jnp.where(q >= 2, -sin, sin)
    cos = jnp.where((q == 1) | (q == 2), -cos, cos)
    return sin, cos


def mm(a, b, contract=((1,), (0,))):
    return lax.dot_general(a, b, (contract, ((), ())), preferred_element_type=F32)


def partner(me, m, n):
    if n & (n - 1):
        return lax.rem(me + m, n)
    to, bit = 0, 1
    while bit < n:
        to = to + bit * lax.rem(me // bit + (m // bit) % 2, 2)
        bit *= 2
    return to


def source_of(me, m, n):
    return lax.rem(me + n - m, n) if n & (n - 1) else partner(me, m, n)


def blocks_of(n, f):
    if n == 1:
        f(0)
    else:
        pl.loop(0, n)(f)


def kernel(
    n_elem, n_buck, node_any, eroded_any, bmap_any, spoint_any, sangle_any, out,
    node, eroded, bmap, spoint, sangle,
    perm, pick, rows, faces, onehot, points, angles, values, seg_t, counts,
    sel0, sel1, parts,
    in_sem, seg_send, seg_recv, cnt_send, cnt_recv, par_send, par_recv,
):
    me = lax.axis_index("elem")
    mb = lax.axis_index("bucket")
    own, segs = sangle.shape[0], sangle.shape[2]
    buckets = own * n_elem
    count = eroded.shape[1]
    jblocks = count // LANES
    blocks = node.shape[1] // BLOCK
    nfaces = SIDES * count
    chunks, wide = parts.shape[1], parts.shape[3]
    mesh_ids = pl.DeviceIdType.MESH

    barrier = pltpu.get_barrier_semaphore()
    for m in range(n_elem - 1, 0, -1):
        to = {"elem": partner(me, m, n_elem)}
        pl.semaphore_signal(barrier, inc=1, device_id=to, device_id_type=mesh_ids)
    for d in range(1, n_buck):
        to = {"bucket": lax.rem(mb + d, n_buck)}
        pl.semaphore_signal(barrier, inc=1, device_id=to, device_id_type=mesh_ids)
    loads = [
        pltpu.make_async_copy(src, dst, in_sem.at[i])
        for i, (src, dst) in enumerate([
            (spoint_any, spoint), (sangle_any, sangle), (eroded_any, eroded),
            (bmap_any, bmap), (node_any, node),
        ])
    ]
    for load in loads:
        load.start()

    col = lax.broadcasted_iota(jnp.int32, (1, BLOCK), 1)
    source = SIDES * (col & (LANES - 1)) + (col // LANES)
    for i in range(BLOCK // 256):
        r = lax.broadcasted_iota(jnp.int32, (256, BLOCK), 0) + i * 256
        perm[i * 256:(i + 1) * 256, :] = jnp.where(r == source, 1.0, 0.0).astype(BF16)

    def seg_copies(m, owner, target):
        at = pl.ds(pl.multiple_of(owner * own, own), own)
        return [
            pltpu.make_async_remote_copy(
                src_ref=src, dst_ref=dst,
                send_sem=seg_send.at[i, m - 1], recv_sem=seg_recv.at[i, m - 1],
                device_id={"elem": target}, device_id_type=mesh_ids,
            )
            for i, (src, dst) in enumerate(
                [(spoint, points.at[:, at]), (sangle, angles.at[at])]
            )
        ]

    loads[0].wait()
    loads[1].wait()
    pl.semaphore_wait(barrier, n_elem + n_buck - 2)
    for m in range(n_elem - 1, 0, -1):
        for c in seg_copies(m, me, partner(me, m, n_elem)):
            c.start()

    loads[2].wait()
    loads[3].wait()
    erode = eroded[...]
    high = lax.broadcasted_iota(jnp.int32, (blocks, count), 0) == erode // LANES
    low = lax.broadcasted_iota(jnp.int32, (LANES, count), 0) == lax.rem(erode, LANES)
    mask = mm(
        jnp.where(high, 1.0, 0.0).astype(BF16), jnp.where(low, 1.0, 0.0).astype(BF16), ((1,), (1,))
    )
    first = SIDES * lax.broadcasted_iota(jnp.int32, (LANES, BLOCK), 0)
    away = lax.broadcasted_iota(jnp.int32, (LANES, BLOCK), 1) - first
    spread = jnp.where((away >= 0) & (away < SIDES), 1.0, 0.0).astype(BF16)
    mask = mm(mask.astype(BF16), spread)

    chunk = min(buckets, LANES)

    def count_block(b):
        iota = lax.broadcasted_iota(jnp.int32, (chunk, LANES), 0) + b * chunk
        total = jnp.zeros((chunk, LANES), F32)
        for r in range(blocks):
            ids = jnp.where(mask[r:r + 1] > 0.5, bmap[:, r * BLOCK:(r + 1) * BLOCK], -1)
            for g in range(SIDES):
                hit = iota == ids[:, g * LANES:(g + 1) * LANES]
                total = total + jnp.where(hit, 1.0, 0.0)
        if chunk < LANES:
            total = jnp.concatenate([total, jnp.zeros((LANES - chunk, LANES), F32)], axis=0)
        sums = mm(jnp.ones((8, LANES), BF16), total.astype(BF16), ((1,), (1,)))
        at = 0 if buckets <= LANES else pl.ds(pl.multiple_of(b * LANES, LANES), LANES)
        if buckets <= LANES:
            counts[me] = sums[0:1]
        else:
            counts[me, :, at] = sums[0:1]

    blocks_of(buckets // chunk, count_block)

    def cnt_copy(m, owner, target):
        return pltpu.make_async_remote_copy(
            src_ref=counts.at[owner], dst_ref=counts.at[owner],
            send_sem=cnt_send.at[m - 1], recv_sem=cnt_recv.at[m - 1],
            device_id={"elem": target}, device_id_type=mesh_ids,
        )

    for m in range(n_elem - 1, 0, -1):
        cnt_copy(m, me, partner(me, m, n_elem)).start()

    for i in range(pick.shape[0] // 256):
        r = lax.broadcasted_iota(jnp.int32, (256, count), 0) + i * 256
        pick[i * 256:(i + 1) * 256, :] = jnp.where(r == erode, 1.0, 0.0).astype(BF16)

    loads[4].wait()
    group = 4
    for g in range(blocks // group):
        stack = []
        for i in range(g * group, (g + 1) * group):
            lanes = slice(i * BLOCK, (i + 1) * BLOCK)
            c = [node[3 * v:3 * v + 3, lanes] for v in range(8)]
            e1, e2 = c[2] - c[0], c[3] - c[1]
            r1 = jnp.concatenate([e1[1:3], e1[0:1]], axis=0)
            r2 = jnp.concatenate([e2[1:3], e2[0:1]], axis=0)
            area = 0.5 * (e1 * r2 - r1 * e2)
            centroid = 0.25 * (((c[0] + c[1]) + c[2]) + c[3])
            velocity = 0.25 * (((c[4] + c[5]) + c[6]) + c[7])
            ids = bmap[:, lanes].astype(F32)
            two = jnp.zeros((2, BLOCK), F32)
            four = jnp.zeros((4, BLOCK), F32)
            first = jnp.concatenate([centroid, area, two], axis=0)
            second = jnp.concatenate([velocity, ids, four], axis=0)
            a, b = split3(first), split3(second)
            stack += [a[0], b[0], a[1], b[1], a[2]]
        apart = mm(jnp.concatenate(stack, axis=0).astype(BF16), perm[...]).astype(BF16)
        for i in range(group):
            at = (g * group + i) * LANES
            for s in range(SIDES):
                rows[s * 40:(s + 1) * 40, at:at + LANES] = apart[
                    i * 40:(i + 1) * 40, s * LANES:(s + 1) * LANES
                ]

    taken = mm(rows[...], pick[...]).astype(BF16)
    stack = []
    for j in range(jblocks):
        lanes = slice(j * LANES, (j + 1) * LANES)
        stack.append(
            jnp.concatenate([taken[s * 40:(s + 1) * 40, lanes] for s in range(SIDES)], axis=1)
        )
    mixed = mm(jnp.concatenate(stack, axis=0), perm[...], ((1,), (1,)))
    for j in range(jblocks):
        t = [mixed[j * 40 + i * 8:j * 40 + i * 8 + 8] for i in range(5)]
        lanes = slice(j * BLOCK, (j + 1) * BLOCK)
        faces[0:8, lanes] = (t[0] + t[2]) + t[4]
        faces[8:16, lanes] = t[1] + t[3]

    def hot_block(b):
        for j in range(nfaces // 512):
            lanes = slice(j * 512, (j + 1) * 512)
            iota = lax.broadcasted_iota(jnp.int32, (chunk, 512), 0) + b * chunk
            hit = iota == faces[11:12, lanes].astype(jnp.int32)
            onehot[pl.ds(b * chunk, chunk), lanes] = jnp.where(hit, 1.0, 0.0).astype(BF16)

    blocks_of(buckets // chunk, hot_block)

    def unfold(owner, p, a):
        at = pl.ds(pl.multiple_of(owner * own, own), own)
        sin0, cos0 = sin_cos(a[:, 0, :])
        sin1, cos1 = sin_cos(a[:, 1, :])
        x, y, z = [SCALE * p[i] for i in range(3)]
        for i, v in enumerate([x, y, z, cos0 * sin1, sin0 * sin1, cos1]):
            values[i, at, :] = v

    unfold(me, spoint[...], sangle[...])
    for m in range(1, n_elem):
        owner = source_of(me, m, n_elem)
        for cp in seg_copies(m, owner, me):
            cp.wait_recv()
        at = pl.ds(pl.multiple_of(owner * own, own), own)
        unfold(owner, points[:, at, :], angles[at])

    chunk = min(buckets, LANES // 2)

    def lay_out(b):
        for i in range(6):
            v = values[i, pl.ds(pl.multiple_of(b * chunk, chunk), chunk), :]
            stack = jnp.concatenate(list(split3(v)) + [jnp.zeros_like(v)], axis=0)
            lanes = pl.ds(pl.multiple_of(b * 4 * chunk, LANES), 4 * chunk)
            seg_t[i * segs:(i + 1) * segs, lanes] = stack.T.astype(BF16)

    blocks_of(buckets // chunk, lay_out)

    for m in range(1, n_elem):
        cnt_copy(m, source_of(me, m, n_elem), me).wait_recv()
    whole = counts[0]
    for i in range(1, n_elem):
        whole = whole + counts[i]
    stiff = (STIFFNESS / SCALE) * lax.rsqrt(jnp.maximum(whole[:, :buckets], 1.0))
    hi, mid, lo = split3(jnp.broadcast_to(stiff, (16, buckets)))
    pieces = []
    for b in range(0, buckets, chunk):
        cut = slice(b, b + chunk)
        pieces += [hi[:, cut], mid[:, cut], lo[:, cut], jnp.zeros((16, chunk), F32)]
    seg_t[6 * segs:6 * segs + 16, :] = jnp.concatenate(pieces, axis=1).astype(BF16)

    half = 256
    steps = nfaces // half

    def select(it, sel):
        hot = onehot[:, pl.ds(pl.multiple_of(it * half, half), half)]
        hot = [hot[b:b + chunk] for b in range(0, buckets, chunk) for _ in range(4)]
        sel[...] = mm(seg_t[...], jnp.concatenate(hot, axis=0))

    def forces(it, c, at, sel):
        for lt in range(half // LANES):
            g = faces[:, pl.ds(pl.multiple_of(it * half + lt * LANES, LANES), LANES)]
            cx, cy, cz, az, ax, ay, _, _, vx, vy, vz = [
                jnp.broadcast_to(g[i:i + 1], (8, LANES)) for i in range(11)
            ]
            cx, cy, cz = SCALE * cx, SCALE * cy, SCALE * cz
            damp = DAMPING / SCALE
            vx, vy, vz = damp * vx, damp * vy, damp * vz
            tile = slice(lt * LANES, (lt + 1) * LANES)
            stf = sel[6 * segs:6 * segs + 8, tile]
            acc = [jnp.zeros((8, LANES), F32) for _ in range(3)]
            for r in range(segs // 8):
                px, py, pz, nx, ny, nz = [
                    sel[q * segs + r * 8:q * segs + r * 8 + 8, tile] for q in range(6)
                ]
                ox, oy, oz = px - cx, py - cy, pz - cz
                dist = ox * ox + oy * oy + oz * oz
                depth = jnp.maximum(ox * nx + oy * ny + oz * nz, 0.0)
                proj = jnp.abs(ax * nx + ay * ny + az * nz)
                push = stf - (vx * nx + vy * ny + vz * nz)
                traction = (jnp.exp2(-dist) * depth) * (push * proj)
                for k, n in enumerate((nx, ny, nz)):
                    acc[k] = acc[k] + traction * n
            for k in range(3):
                total = jnp.sum(acc[k], axis=0, keepdims=True)
                parts[mb, c, k:k + 1, at + lt * LANES:at + (lt + 1) * LANES] = total

    def par_copy(c, d, owner, target):
        return pltpu.make_async_remote_copy(
            src_ref=parts.at[owner, c], dst_ref=parts.at[owner, c],
            send_sem=par_send.at[c, d - 1], recv_sem=par_recv.at[c, d - 1],
            device_id={"bucket": target}, device_id_type=mesh_ids,
        )

    select(0, sel0)

    def step(c, carry):
        it = 2 * c
        select(it + 1, sel1)
        forces(it, c, 0, sel0)
        select(lax.rem(it + 2, steps), sel0)
        forces(it + 1, c, half, sel1)
        for d in range(1, n_buck):
            par_copy(c, d, mb, lax.rem(mb + d, n_buck)).start()
        return carry

    lax.fori_loop(0, chunks, step, 0)

    for c in range(chunks):
        for d in range(1, n_buck):
            par_copy(c, d, lax.rem(mb + n_buck - d, n_buck), mb).wait_recv()
        force = parts[0, c]
        for i in range(1, n_buck):
            force = force + parts[i, c]
        out[:, c * wide:(c + 1) * wide] = force

    for m in range(1, n_elem):
        for cp in seg_copies(m, me, partner(me, m, n_elem)):
            cp.wait_send()
        cnt_copy(m, me, partner(me, m, n_elem)).wait_send()
    for c in range(chunks):
        for d in range(1, n_buck):
            par_copy(c, d, mb, lax.rem(mb + d, n_buck)).wait_send()


def local(n_elem, n_buck, node_data, eroded, bucket_map, seg_point, seg_angle):
    own, _, segs = seg_point.shape
    buckets = own * n_elem
    count = eroded.shape[0]
    elems = node_data.shape[1] // SIDES
    nfaces = SIDES * count
    wide = 512
    dma = pltpu.SemaphoreType.DMA
    points = seg_point.transpose(1, 0, 2)
    operands = (node_data, eroded[None, :], bucket_map[None, :], points, seg_angle)
    scratch = [
        (node_data.shape, F32),
        ((1, count), jnp.int32),
        ((1, node_data.shape[1]), jnp.int32),
        ((3, own, segs), F32),
        ((own, 2, segs), F32),
        ((BLOCK, BLOCK), BF16),
        ((elems, count), BF16),
        ((SIDES * 40, elems), BF16),
        ((16, nfaces), F32),
        ((buckets, nfaces), BF16),
        ((3, buckets, segs), F32),
        ((buckets, 2, segs), F32),
        ((6, buckets, segs), F32),
        ((6 * segs + 16, 4 * buckets), BF16),
        ((n_elem, 1, max(buckets, LANES)), F32),
        ((6 * segs + 16, 256), F32),
        ((6 * segs + 16, 256), F32),
        ((n_buck, nfaces // wide, 3, wide), F32),
    ]
    need = sum(math.prod(shape) * jnp.dtype(kind).itemsize for shape, kind in scratch)
    return pl.pallas_call(
        functools.partial(kernel, n_elem, n_buck),
        out_shape=jax.ShapeDtypeStruct((3, nfaces), F32),
        in_specs=[pl.BlockSpec(memory_space=pltpu.HBM)] * 5,
        out_specs=pl.BlockSpec(memory_space=pltpu.VMEM),
        scratch_shapes=[pltpu.VMEM(shape, kind) for shape, kind in scratch]
        + [
            dma((5,)),
            dma((2, n_elem - 1)),
            dma((2, n_elem - 1)),
            dma((n_elem - 1,)),
            dma((n_elem - 1,)),
            dma((nfaces // wide, n_buck - 1)),
            dma((nfaces // wide, n_buck - 1)),
        ],
        compiler_params=pltpu.CompilerParams(
            collective_id=0, has_side_effects=True,
            vmem_limit_bytes=need + 12 * 1024 * 1024,
        ),
        name="contact",
    )(*[pltpu.with_memory_space_constraint(x, pltpu.HBM) for x in operands])


def solution(mesh):
    in_specs = (
        P(None, "elem"),
        P("elem"),
        P("elem"),
        P("elem", None, "bucket"),
        P("elem", None, "bucket"),
    )
    body = functools.partial(local, mesh.shape["elem"], mesh.shape["bucket"])
    return jax.shard_map(
        body, mesh=mesh, in_specs=in_specs, out_specs=P(None, "elem"), check_vma=False
    )
```

time: 21.9 us -> 19.2 us (0.88)
  Pallas kernels: 20.2 us -> 18.4 us
  local copies, waits for them, and re-layouts: 1.43 us -> 0.62 us
    pallas_call x1, Pallas kernels: 20.2 us -> 18.4 us  [local(): pl.pallas_call(functools.partial(kernel, n_elem, n_buck), out_shape=jax.S...]
    unnamed x1, local copies, waits for them, and re-layouts: 1.43 us -> 0.62 us
where the time goes in v1:
time: 19.2 us; the launch traced here: 19 us
  Pallas kernels  18.4 us (96%)
  local copies, waits for them, and re-layouts  0.62 us (3%)
    pallas_call x1, Pallas kernels, local(): pl.pallas_call(functools.partial(kernel, n_elem, n_buck), out_shape=jax.S...  18.4 us
    unnamed x1, local copies, waits for them, and re-layouts  0.62 us

profile of v1, /device:TPU:0, one launch (start us, length us, event | category | flops | bytes accessed | tf_op | source)
XLA Modules:
  0.0 19.0 jit_solution(15193995759613890313)
XLA Ops:
  0.0 18.4 %contact.1 = f32[3,3072]{1,0:T(4,128)S(1)} custom-call(f32[24,12288]{1,0:T(8,128)} %node_any.1, s32[1,512]{1,0:T(1,128)} %bitcast.5, s32[1,12288]{1,0:T(1,128)} %bitcast.3, f32[3,8,128]{2,1,0:T(8,128)} %bitcast.4, f32[8,2,128]{2,1,0:T(2,128)} %sangle_any.1), custom_call_target="tpu_custom_call" | custom-call | tf_op jit(solution)/shard_map/contact/pallas_call | solution.py:376
  18.4 0.6 %copy.7 = f32[3,3072]{1,0:T(4,128)} copy(f32[3,3072]{1,0:T(4,128)S(1)} %contact.1) | data formatting | bytes 73728

commit v2 on v1

--- a/solution.py
+++ b/solution.py
@@ -70,35 +70,48 @@
 
 def kernel(
     n_elem, n_buck, node_any, eroded_any, bmap_any, spoint_any, sangle_any, out,
-    node, eroded, bmap, spoint, sangle,
-    perm, pick, rows, faces, onehot, points, angles, values, seg_t, counts,
+    node, eroded, bmap, perm, pick, rows, faces, onehot, table, values, seg_t, counts,
     sel0, sel1, parts,
-    in_sem, seg_send, seg_recv, cnt_send, cnt_recv, par_send, par_recv,
+    in_sem, seg_send, seg_recv, cnt_sem, par_send, par_recv, ready, go,
 ):
     me = lax.axis_index("elem")
     mb = lax.axis_index("bucket")
-    own, segs = sangle.shape[0], sangle.shape[2]
-    buckets = own * n_elem
+    buckets, segs = table.shape[1:]
+    own = buckets // n_elem
     count = eroded.shape[1]
     jblocks = count // LANES
     blocks = node.shape[1] // BLOCK
     nfaces = SIDES * count
-    chunks, wide = parts.shape[1], parts.shape[3]
+    chunks, wide = parts.shape[0], parts.shape[3]
     mesh_ids = pl.DeviceIdType.MESH
 
     barrier = pltpu.get_barrier_semaphore()
     for m in range(n_elem - 1, 0, -1):
         to = {"elem": partner(me, m, n_elem)}
         pl.semaphore_signal(barrier, inc=1, device_id=to, device_id_type=mesh_ids)
-    for d in range(1, n_buck):
-        to = {"bucket": lax.rem(mb + d, n_buck)}
-        pl.semaphore_signal(barrier, inc=1, device_id=to, device_id_type=mesh_ids)
+
+    leads = me == 0
+
+    @pl.when(leads)
+    def _():
+        for d in range(1, n_buck):
+            to = {"bucket": lax.rem(mb + d, n_buck)}
+            pl.semaphore_signal(barrier, inc=1, device_id=to, device_id_type=mesh_ids)
+
+    def held(owner):
+        return table.at[:, pl.ds(pl.multiple_of(owner * own, own), own)]
+
+    mine = pl.ds(pl.multiple_of(me * own, own), own)
     loads = [
         pltpu.make_async_copy(src, dst, in_sem.at[i])
-        for i, (src, dst) in enumerate([
-            (spoint_any, spoint), (sangle_any, sangle), (eroded_any, eroded),
-            (bmap_any, bmap), (node_any, node),
-        ])
+        for i, src, dst in [
+            (0, spoint_any, table.at[0:3, mine]),
+            (0, sangle_any.at[:, 0], table.at[3, mine]),
+            (0, sangle_any.at[:, 1], table.at[4, mine]),
+            (1, eroded_any, eroded),
+            (2, bmap_any, bmap),
+            (3, node_any, node),
+        ]
     ]
     for load in loads:
         load.start()
@@ -109,28 +122,27 @@
         r = lax.broadcasted_iota(jnp.int32, (256, BLOCK), 0) + i * 256
         perm[i * 256:(i + 1) * 256, :] = jnp.where(r == source, 1.0, 0.0).astype(BF16)
 
-    def seg_copies(m, owner, target):
-        at = pl.ds(pl.multiple_of(owner * own, own), own)
-        return [
-            pltpu.make_async_remote_copy(
-                src_ref=src, dst_ref=dst,
-                send_sem=seg_send.at[i, m - 1], recv_sem=seg_recv.at[i, m - 1],
-                device_id={"elem": target}, device_id_type=mesh_ids,
-            )
-            for i, (src, dst) in enumerate(
-                [(spoint, points.at[:, at]), (sangle, angles.at[at])]
-            )
-        ]
-
-    loads[0].wait()
-    loads[1].wait()
-    pl.semaphore_wait(barrier, n_elem + n_buck - 2)
+    def seg_copy(m, owner, target):
+        return pltpu.make_async_remote_copy(
+            src_ref=held(owner), dst_ref=held(owner),
+            send_sem=seg_send, recv_sem=seg_recv.at[m - 1],
+            device_id={"elem": target}, device_id_type=mesh_ids,
+        )
+
+    pltpu.make_async_copy(held(me), held(me), in_sem.at[0]).wait()
+    pl.semaphore_wait(barrier, n_elem - 1 + jnp.where(leads, n_buck - 1, 0))
+
     for m in range(n_elem - 1, 0, -1):
-        for c in seg_copies(m, me, partner(me, m, n_elem)):
-            c.start()
-
-    loads[2].wait()
+        seg_copy(m, me, partner(me, m, n_elem)).start()
+
+    @pl.when(leads)
+    def _():
+        for d in range(1, n_buck):
+            to = {"bucket": lax.rem(mb + d, n_buck)}
+            pl.semaphore_signal(ready, inc=1, device_id=to, device_id_type=mesh_ids)
+
     loads[3].wait()
+    loads[4].wait()
     erode = eroded[...]
     high = lax.broadcasted_iota(jnp.int32, (blocks, count), 0) == erode // LANES
     low = lax.broadcasted_iota(jnp.int32, (LANES, count), 0) == lax.rem(erode, LANES)
@@ -163,21 +175,21 @@
 
     blocks_of(buckets // chunk, count_block)
 
-    def cnt_copy(m, owner, target):
+    def cnt_copy(at, target):
         return pltpu.make_async_remote_copy(
-            src_ref=counts.at[owner], dst_ref=counts.at[owner],
-            send_sem=cnt_send.at[m - 1], recv_sem=cnt_recv.at[m - 1],
+            src_ref=counts.at[at], dst_ref=counts.at[at],
+            send_sem=cnt_sem.at[0], recv_sem=cnt_sem.at[1],
             device_id={"elem": target}, device_id_type=mesh_ids,
         )
 
     for m in range(n_elem - 1, 0, -1):
-        cnt_copy(m, me, partner(me, m, n_elem)).start()
+        cnt_copy(me, partner(me, m, n_elem)).start()
 
     for i in range(pick.shape[0] // 256):
         r = lax.broadcasted_iota(jnp.int32, (256, count), 0) + i * 256
         pick[i * 256:(i + 1) * 256, :] = jnp.where(r == erode, 1.0, 0.0).astype(BF16)
 
-    loads[4].wait()
+    loads[5].wait()
     group = 4
     for g in range(blocks // group):
         stack = []
@@ -205,6 +217,13 @@
                     i * 40:(i + 1) * 40, s * LANES:(s + 1) * LANES
                 ]
 
+    @pl.when(leads)
+    def _():
+        pl.semaphore_wait(ready, n_buck - 1)
+        for m in range(n_elem - 1, 0, -1):
+            to = {"elem": partner(me, m, n_elem)}
+            pl.semaphore_signal(go, inc=1, device_id=to, device_id_type=mesh_ids)
+
     taken = mm(rows[...], pick[...]).astype(BF16)
     stack = []
     for j in range(jblocks):
@@ -228,21 +247,20 @@
 
     blocks_of(buckets // chunk, hot_block)
 
-    def unfold(owner, p, a):
+    def unfold(owner):
         at = pl.ds(pl.multiple_of(owner * own, own), own)
-        sin0, cos0 = sin_cos(a[:, 0, :])
-        sin1, cos1 = sin_cos(a[:, 1, :])
-        x, y, z = [SCALE * p[i] for i in range(3)]
+        sin0, cos0 = sin_cos(table[3, at, :])
+        sin1, cos1 = sin_cos(table[4, at, :])
+        x, y, z = [SCALE * table[i, at, :] for i in range(3)]
         for i, v in enumerate([x, y, z, cos0 * sin1, sin0 * sin1, cos1]):
             values[i, at, :] = v
 
-    unfold(me, spoint[...], sangle[...])
+    unfold(me)
     for m in range(1, n_elem):
         owner = source_of(me, m, n_elem)
-        for cp in seg_copies(m, owner, me):
-            cp.wait_recv()
-        at = pl.ds(pl.multiple_of(owner * own, own), own)
-        unfold(owner, points[:, at, :], angles[at])
+        seg_copy(m, owner, me).wait_recv()
+        unfold(owner)
+    cnt_copy(pl.ds(0, n_elem - 1), me).wait_recv()
 
     chunk = min(buckets, LANES // 2)
 
@@ -255,8 +273,6 @@
 
     blocks_of(buckets // chunk, lay_out)
 
-    for m in range(1, n_elem):
-        cnt_copy(m, source_of(me, m, n_elem), me).wait_recv()
     whole = counts[0]
     for i in range(1, n_elem):
         whole = whole + counts[i]
@@ -302,12 +318,12 @@
                     acc[k] = acc[k] + traction * n
             for k in range(3):
                 total = jnp.sum(acc[k], axis=0, keepdims=True)
-                parts[mb, c, k:k + 1, at + lt * LANES:at + (lt + 1) * LANES] = total
-
-    def par_copy(c, d, owner, target):
+                parts[c, mb, k:k + 1, at + lt * LANES:at + (lt + 1) * LANES] = total
+
+    def par_copy(at, who, some, target):
         return pltpu.make_async_remote_copy(
-            src_ref=parts.at[owner, c], dst_ref=parts.at[owner, c],
-            send_sem=par_send.at[c, d - 1], recv_sem=par_recv.at[c, d - 1],
+            src_ref=parts.at[at, who], dst_ref=parts.at[at, who],
+            send_sem=par_send, recv_sem=par_recv.at[some],
             device_id={"bucket": target}, device_id_type=mesh_ids,
         )
 
@@ -320,26 +336,33 @@
         select(lax.rem(it + 2, steps), sel0)
         forces(it + 1, c, half, sel1)
         for d in range(1, n_buck):
-            par_copy(c, d, mb, lax.rem(mb + d, n_buck)).start()
+            par_copy(c, mb, c // (chunks - 1), lax.rem(mb + d, n_buck)).start()
         return carry
 
+    @pl.when(jnp.logical_not(leads))
+    def _():
+        pl.semaphore_wait(go, 1)
+
     lax.fori_loop(0, chunks, step, 0)
 
-    for c in range(chunks):
-        for d in range(1, n_buck):
-            par_copy(c, d, lax.rem(mb + n_buck - d, n_buck), mb).wait_recv()
-        force = parts[0, c]
+    others = pl.ds(0, n_buck - 1)
+
+    def finish(c):
+        force = parts[c, 0]
         for i in range(1, n_buck):
-            force = force + parts[i, c]
+            force = force + parts[c, i]
         out[:, c * wide:(c + 1) * wide] = force
 
-    for m in range(1, n_elem):
-        for cp in seg_copies(m, me, partner(me, m, n_elem)):
-            cp.wait_send()
-        cnt_copy(m, me, partner(me, m, n_elem)).wait_send()
-    for c in range(chunks):
-        for d in range(1, n_buck):
-            par_copy(c, d, mb, lax.rem(mb + d, n_buck)).wait_send()
+    par_copy(pl.ds(0, chunks - 1), others, 0, mb).wait_recv()
+    for c in range(chunks - 1):
+        finish(c)
+    par_copy(pl.ds(chunks - 1, 1), others, 1, mb).wait_recv()
+    finish(chunks - 1)
+
+    rest = pl.ds(0, own * (n_elem - 1))
+    pltpu.make_async_copy(table.at[:, rest], table.at[:, rest], seg_send).wait()
+    cnt_copy(pl.ds(0, n_elem - 1), me).wait_send()
+    par_copy(pl.ds(0, chunks), others, 0, mb).wait_send()
 
 
 def local(n_elem, n_buck, node_data, eroded, bucket_map, seg_point, seg_angle):
@@ -356,21 +379,18 @@
         (node_data.shape, F32),
         ((1, count), jnp.int32),
         ((1, node_data.shape[1]), jnp.int32),
-        ((3, own, segs), F32),
-        ((own, 2, segs), F32),
         ((BLOCK, BLOCK), BF16),
         ((elems, count), BF16),
         ((SIDES * 40, elems), BF16),
         ((16, nfaces), F32),
         ((buckets, nfaces), BF16),
-        ((3, buckets, segs), F32),
-        ((buckets, 2, segs), F32),
+        ((5, buckets, segs), F32),
         ((6, buckets, segs), F32),
         ((6 * segs + 16, 4 * buckets), BF16),
         ((n_elem, 1, max(buckets, LANES)), F32),
         ((6 * segs + 16, 256), F32),
         ((6 * segs + 16, 256), F32),
-        ((n_buck, nfaces // wide, 3, wide), F32),
+        ((nfaces // wide, n_buck, 3, wide), F32),
     ]
     need = sum(math.prod(shape) * jnp.dtype(kind).itemsize for shape, kind in scratch)
     return pl.pallas_call(
@@ -380,13 +400,14 @@
         out_specs=pl.BlockSpec(memory_space=pltpu.VMEM),
         scratch_shapes=[pltpu.VMEM(shape, kind) for shape, kind in scratch]
         + [
-            dma((5,)),
-            dma((2, n_elem - 1)),
-            dma((2, n_elem - 1)),
+            dma((4,)),
+            dma,
             dma((n_elem - 1,)),
-            dma((n_elem - 1,)),
-            dma((nfaces // wide, n_buck - 1)),
-            dma((nfaces // wide, n_buck - 1)),
+            dma((2,)),
+            dma,
+            dma((2,)),
+            pltpu.SemaphoreType.REGULAR,
+            pltpu.SemaphoreType.REGULAR,
         ],
         compiler_params=pltpu.CompilerParams(
             collective_id=0, has_side_effects=True,

time: 19.2 us -> 18.3 us (0.953)
  Pallas kernels: 18.4 us -> 17.5 us
    pallas_call x1, Pallas kernels: 18.4 us -> 17.5 us  [local(): pl.pallas_call(functools.partial(kernel, n_elem, n_buck), out_shape=jax.S...]
where the time goes in v2:
time: 18.3 us; the launch traced here: 18.1 us
  Pallas kernels  17.5 us (96%)
  local copies, waits for them, and re-layouts  0.62 us (3%)
    pallas_call x1, Pallas kernels, local(): pl.pallas_call(functools.partial(kernel, n_elem, n_buck), out_shape=jax.S...  17.5 us
    unnamed x1, local copies, waits for them, and re-layouts  0.62 us

profile of v2, /device:TPU:0, one launch (start us, length us, event | category | flops | bytes accessed | tf_op | source)
XLA Modules:
  0.0 18.1 jit_solution(660541394260943510)
XLA Ops:
  0.0 17.5 %contact.1 = f32[3,3072]{1,0:T(4,128)S(1)} custom-call(f32[24,12288]{1,0:T(8,128)} %node_any.1, s32[1,512]{1,0:T(1,128)} %bitcast.5, s32[1,12288]{1,0:T(1,128)} %bitcast.3, f32[3,8,128]{2,1,0:T(8,128)} %bitcast.4, f32[8,2,128]{2,1,0:T(2,128)} %sangle_any.1), custom_call_target="tpu_custom_call" | custom-call | tf_op jit(solution)/shard_map/contact/pallas_call | solution.py:396
  17.5 0.6 %copy.7 = f32[3,3072]{1,0:T(4,128)} copy(f32[3,3072]{1,0:T(4,128)S(1)} %contact.1) | data formatting | bytes 73728

commit v3 on v2

--- a/solution.py
+++ b/solution.py
@@ -61,6 +61,10 @@
     return lax.rem(me + n - m, n) if n & (n - 1) else partner(me, m, n)
 
 
+def other(me, u):
+    return u + jnp.where(u >= me, 1, 0)
+
+
 def blocks_of(n, f):
     if n == 1:
         f(0)
@@ -70,7 +74,7 @@
 
 def kernel(
     n_elem, n_buck, node_any, eroded_any, bmap_any, spoint_any, sangle_any, out,
-    node, eroded, bmap, perm, pick, rows, faces, onehot, table, values, seg_t, counts,
+    node, eroded, bmap, perm, spread, pick, rows, faces, onehot, table, values, seg_t, counts,
     sel0, sel1, parts,
     in_sem, seg_send, seg_recv, cnt_sem, par_send, par_recv, ready, go,
 ):
@@ -86,8 +90,8 @@
     mesh_ids = pl.DeviceIdType.MESH
 
     barrier = pltpu.get_barrier_semaphore()
-    for m in range(n_elem - 1, 0, -1):
-        to = {"elem": partner(me, m, n_elem)}
+    for u in range(n_elem - 1):
+        to = {"elem": other(me, u)}
         pl.semaphore_signal(barrier, inc=1, device_id=to, device_id_type=mesh_ids)
 
     leads = me == 0
@@ -122,58 +126,121 @@
         r = lax.broadcasted_iota(jnp.int32, (256, BLOCK), 0) + i * 256
         perm[i * 256:(i + 1) * 256, :] = jnp.where(r == source, 1.0, 0.0).astype(BF16)
 
-    def seg_copy(m, owner, target):
+    first = SIDES * lax.broadcasted_iota(jnp.int32, (LANES, BLOCK), 0)
+    away = lax.broadcasted_iota(jnp.int32, (LANES, BLOCK), 1) - first
+    spread[...] = jnp.where((away >= 0) & (away < SIDES), 1.0, 0.0).astype(BF16)
+
+    def seg_copy(owner, target):
         return pltpu.make_async_remote_copy(
             src_ref=held(owner), dst_ref=held(owner),
-            send_sem=seg_send, recv_sem=seg_recv.at[m - 1],
+            send_sem=seg_send, recv_sem=seg_recv.at[owner - jnp.where(owner > target, 1, 0)],
             device_id={"elem": target}, device_id_type=mesh_ids,
         )
 
+    chunk = min(buckets, LANES)
+
+    def tally():
+        loads[3].wait()
+        loads[4].wait()
+        erode = eroded[...]
+        high = lax.broadcasted_iota(jnp.int32, (blocks, count), 0) == erode // LANES
+        low = lax.broadcasted_iota(jnp.int32, (LANES, count), 0) == lax.rem(erode, LANES)
+        mask = mm(
+            jnp.where(high, 1.0, 0.0).astype(BF16), jnp.where(low, 1.0, 0.0).astype(BF16), ((1,), (1,))
+        )
+        mask = mm(mask.astype(BF16), spread[...])
+
+        def count_block(b):
+            iota = lax.broadcasted_iota(jnp.int32, (chunk, LANES), 0) + b * chunk
+            total = jnp.zeros((chunk, LANES), F32)
+            for r in range(blocks):
+                ids = jnp.where(mask[r:r + 1] > 0.5, bmap[:, r * BLOCK:(r + 1) * BLOCK], -1)
+                for g in range(SIDES):
+                    hit = iota == ids[:, g * LANES:(g + 1) * LANES]
+                    total = total + jnp.where(hit, 1.0, 0.0)
+            if chunk < LANES:
+                total = jnp.concatenate([total, jnp.zeros((LANES - chunk, LANES), F32)], axis=0)
+            sums = mm(jnp.ones((8, LANES), BF16), total.astype(BF16), ((1,), (1,)))
+            at = 0 if buckets <= LANES else pl.ds(pl.multiple_of(b * LANES, LANES), LANES)
+            if buckets <= LANES:
+                counts[me] = sums[0:1]
+            else:
+                counts[me, :, at] = sums[0:1]
+
+        blocks_of(buckets // chunk, count_block)
+
+    def gather():
+        for i in range(pick.shape[0] // 256):
+            r = lax.broadcasted_iota(jnp.int32, (256, count), 0) + i * 256
+            pick[i * 256:(i + 1) * 256, :] = jnp.where(r == eroded[...], 1.0, 0.0).astype(BF16)
+
+        loads[5].wait()
+        group = 4
+        for g in range(blocks // group):
+            stack = []
+            for i in range(g * group, (g + 1) * group):
+                lanes = slice(i * BLOCK, (i + 1) * BLOCK)
+                c = [node[3 * v:3 * v + 3, lanes] for v in range(8)]
+                e1, e2 = c[2] - c[0], c[3] - c[1]
+                r1 = jnp.concatenate([e1[1:3], e1[0:1]], axis=0)
+                r2 = jnp.concatenate([e2[1:3], e2[0:1]], axis=0)
+                area = 0.5 * (e1 * r2 - r1 * e2)
+                centroid = 0.25 * (((c[0] + c[1]) + c[2]) + c[3])
+                velocity = 0.25 * (((c[4] + c[5]) + c[6]) + c[7])
+                ids = bmap[:, lanes].astype(F32)
+                two = jnp.zeros((2, BLOCK), F32)
+                four = jnp.zeros((4, BLOCK), F32)
+                first = jnp.concatenate([centroid, area, two], axis=0)
+                second = jnp.concatenate([velocity, ids, four], axis=0)
+                a, b = split3(first), split3(second)
+                stack += [a[0], b[0], a[1], b[1], a[2]]
+            apart = mm(jnp.concatenate(stack, axis=0).astype(BF16), perm[...]).astype(BF16)
+            for i in range(group):
+                at = (g * group + i) * LANES
+                for s in range(SIDES):
+                    rows[s * 40:(s + 1) * 40, at:at + LANES] = apart[
+                        i * 40:(i + 1) * 40, s * LANES:(s + 1) * LANES
+                    ]
+
+        taken = mm(rows[...], pick[...]).astype(BF16)
+        stack = []
+        for j in range(jblocks):
+            lanes = slice(j * LANES, (j + 1) * LANES)
+            stack.append(
+                jnp.concatenate([taken[s * 40:(s + 1) * 40, lanes] for s in range(SIDES)], axis=1)
+            )
+        mixed = mm(jnp.concatenate(stack, axis=0), perm[...], ((1,), (1,)))
+        for j in range(jblocks):
+            t = [mixed[j * 40 + i * 8:j * 40 + i * 8 + 8] for i in range(5)]
+            lanes = slice(j * BLOCK, (j + 1) * BLOCK)
+            faces[0:8, lanes] = (t[0] + t[2]) + t[4]
+            faces[8:16, lanes] = t[1] + t[3]
+
+        def hot_block(b):
+            for j in range(nfaces // 512):
+                lanes = slice(j * 512, (j + 1) * 512)
+                iota = lax.broadcasted_iota(jnp.int32, (chunk, 512), 0) + b * chunk
+                hit = iota == faces[11:12, lanes].astype(jnp.int32)
+                onehot[pl.ds(b * chunk, chunk), lanes] = jnp.where(hit, 1.0, 0.0).astype(BF16)
+
+        blocks_of(buckets // chunk, hot_block)
+
+    @pl.when(leads)
+    def _():
+        tally()
+        gather()
+
     pltpu.make_async_copy(held(me), held(me), in_sem.at[0]).wait()
     pl.semaphore_wait(barrier, n_elem - 1 + jnp.where(leads, n_buck - 1, 0))
 
-    for m in range(n_elem - 1, 0, -1):
-        seg_copy(m, me, partner(me, m, n_elem)).start()
+    for u in range(n_elem - 1):
+        seg_copy(me, other(me, u)).start()
 
     @pl.when(leads)
     def _():
         for d in range(1, n_buck):
             to = {"bucket": lax.rem(mb + d, n_buck)}
             pl.semaphore_signal(ready, inc=1, device_id=to, device_id_type=mesh_ids)
-
-    loads[3].wait()
-    loads[4].wait()
-    erode = eroded[...]
-    high = lax.broadcasted_iota(jnp.int32, (blocks, count), 0) == erode // LANES
-    low = lax.broadcasted_iota(jnp.int32, (LANES, count), 0) == lax.rem(erode, LANES)
-    mask = mm(
-        jnp.where(high, 1.0, 0.0).astype(BF16), jnp.where(low, 1.0, 0.0).astype(BF16), ((1,), (1,))
-    )
-    first = SIDES * lax.broadcasted_iota(jnp.int32, (LANES, BLOCK), 0)
-    away = lax.broadcasted_iota(jnp.int32, (LANES, BLOCK), 1) - first
-    spread = jnp.where((away >= 0) & (away < SIDES), 1.0, 0.0).astype(BF16)
-    mask = mm(mask.astype(BF16), spread)
-
-    chunk = min(buckets, LANES)
-
-    def count_block(b):
-        iota = lax.broadcasted_iota(jnp.int32, (chunk, LANES), 0) + b * chunk
-        total = jnp.zeros((chunk, LANES), F32)
-        for r in range(blocks):
-            ids = jnp.where(mask[r:r + 1] > 0.5, bmap[:, r * BLOCK:(r + 1) * BLOCK], -1)
-            for g in range(SIDES):
-                hit = iota == ids[:, g * LANES:(g + 1) * LANES]
-                total = total + jnp.where(hit, 1.0, 0.0)
-        if chunk < LANES:
-            total = jnp.concatenate([total, jnp.zeros((LANES - chunk, LANES), F32)], axis=0)
-        sums = mm(jnp.ones((8, LANES), BF16), total.astype(BF16), ((1,), (1,)))
-        at = 0 if buckets <= LANES else pl.ds(pl.multiple_of(b * LANES, LANES), LANES)
-        if buckets <= LANES:
-            counts[me] = sums[0:1]
-        else:
-            counts[me, :, at] = sums[0:1]
-
-    blocks_of(buckets // chunk, count_block)
 
     def cnt_copy(at, target):
         return pltpu.make_async_remote_copy(
@@ -182,70 +249,23 @@
             device_id={"elem": target}, device_id_type=mesh_ids,
         )
 
-    for m in range(n_elem - 1, 0, -1):
-        cnt_copy(me, partner(me, m, n_elem)).start()
-
-    for i in range(pick.shape[0] // 256):
-        r = lax.broadcasted_iota(jnp.int32, (256, count), 0) + i * 256
-        pick[i * 256:(i + 1) * 256, :] = jnp.where(r == erode, 1.0, 0.0).astype(BF16)
-
-    loads[5].wait()
-    group = 4
-    for g in range(blocks // group):
-        stack = []
-        for i in range(g * group, (g + 1) * group):
-            lanes = slice(i * BLOCK, (i + 1) * BLOCK)
-            c = [node[3 * v:3 * v + 3, lanes] for v in range(8)]
-            e1, e2 = c[2] - c[0], c[3] - c[1]
-            r1 = jnp.concatenate([e1[1:3], e1[0:1]], axis=0)
-            r2 = jnp.concatenate([e2[1:3], e2[0:1]], axis=0)
-            area = 0.5 * (e1 * r2 - r1 * e2)
-            centroid = 0.25 * (((c[0] + c[1]) + c[2]) + c[3])
-            velocity = 0.25 * (((c[4] + c[5]) + c[6]) + c[7])
-            ids = bmap[:, lanes].astype(F32)
-            two = jnp.zeros((2, BLOCK), F32)
-            four = jnp.zeros((4, BLOCK), F32)
-            first = jnp.concatenate([centroid, area, two], axis=0)
-            second = jnp.concatenate([velocity, ids, four], axis=0)
-            a, b = split3(first), split3(second)
-            stack += [a[0], b[0], a[1], b[1], a[2]]
-        apart = mm(jnp.concatenate(stack, axis=0).astype(BF16), perm[...]).astype(BF16)
-        for i in range(group):
-            at = (g * group + i) * LANES
-            for s in range(SIDES):
-                rows[s * 40:(s + 1) * 40, at:at + LANES] = apart[
-                    i * 40:(i + 1) * 40, s * LANES:(s + 1) * LANES
-                ]
+    @pl.when(jnp.logical_not(leads))
+    def _():
+        tally()
+
+    for u in range(n_elem - 1):
+        cnt_copy(me, other(me, u)).start()
+
+    @pl.when(jnp.logical_not(leads))
+    def _():
+        gather()
 
     @pl.when(leads)
     def _():
         pl.semaphore_wait(ready, n_buck - 1)
-        for m in range(n_elem - 1, 0, -1):
-            to = {"elem": partner(me, m, n_elem)}
+        for u in range(n_elem - 1):
+            to = {"elem": other(me, u)}
             pl.semaphore_signal(go, inc=1, device_id=to, device_id_type=mesh_ids)
-
-    taken = mm(rows[...], pick[...]).astype(BF16)
-    stack = []
-    for j in range(jblocks):
-        lanes = slice(j * LANES, (j + 1) * LANES)
-        stack.append(
-            jnp.concatenate([taken[s * 40:(s + 1) * 40, lanes] for s in range(SIDES)], axis=1)
-        )
-    mixed = mm(jnp.concatenate(stack, axis=0), perm[...], ((1,), (1,)))
-    for j in range(jblocks):
-        t = [mixed[j * 40 + i * 8:j * 40 + i * 8 + 8] for i in range(5)]
-        lanes = slice(j * BLOCK, (j + 1) * BLOCK)
-        faces[0:8, lanes] = (t[0] + t[2]) + t[4]
-        faces[8:16, lanes] = t[1] + t[3]
-
-    def hot_block(b):
-        for j in range(nfaces // 512):
-            lanes = slice(j * 512, (j + 1) * 512)
-            iota = lax.broadcasted_iota(jnp.int32, (chunk, 512), 0) + b * chunk
-            hit = iota == faces[11:12, lanes].astype(jnp.int32)
-            onehot[pl.ds(b * chunk, chunk), lanes] = jnp.where(hit, 1.0, 0.0).astype(BF16)
-
-    blocks_of(buckets // chunk, hot_block)
 
     def unfold(owner):
         at = pl.ds(pl.multiple_of(owner * own, own), own)
@@ -258,7 +278,7 @@
     unfold(me)
     for m in range(1, n_elem):
         owner = source_of(me, m, n_elem)
-        seg_copy(m, owner, me).wait_recv()
+        seg_copy(owner, me).wait_recv()
         unfold(owner)
     cnt_copy(pl.ds(0, n_elem - 1), me).wait_recv()
 
@@ -335,8 +355,8 @@
         forces(it, c, 0, sel0)
         select(lax.rem(it + 2, steps), sel0)
         forces(it + 1, c, half, sel1)
-        for d in range(1, n_buck):
-            par_copy(c, mb, c // (chunks - 1), lax.rem(mb + d, n_buck)).start()
+        for m in sorted(range(1, n_buck), key=lambda m: m == 1):
+            par_copy(c, mb, c // (chunks - 1), partner(mb, m, n_buck)).start()
         return carry
 
     @pl.when(jnp.logical_not(leads))
@@ -380,6 +400,7 @@
         ((1, count), jnp.int32),
         ((1, node_data.shape[1]), jnp.int32),
         ((BLOCK, BLOCK), BF16),
+        ((LANES, BLOCK), BF16),
         ((elems, count), BF16),
         ((SIDES * 40, elems), BF16),
         ((16, nfaces), F32),

time: 18.3 us -> 18.1 us (0.989)
  Pallas kernels: 17.5 us -> 17.3 us
    pallas_call x1, Pallas kernels: 17.5 us -> 17.3 us  [local(): pl.pallas_call(functools.partial(kernel, n_elem, n_buck), out_shape=jax.S...]
where the time goes in v3:
time: 18.1 us; the launch traced here: 17.9 us
  Pallas kernels  17.3 us (96%)
  local copies, waits for them, and re-layouts  0.62 us (3%)
    pallas_call x1, Pallas kernels, local(): pl.pallas_call(functools.partial(kernel, n_elem, n_buck), out_shape=jax.S...  17.3 us
    unnamed x1, local copies, waits for them, and re-layouts  0.62 us

profile of v3, /device:TPU:0, one launch (start us, length us, event | category | flops | bytes accessed | tf_op | source)
XLA Modules:
  0.0 17.9 jit_solution(14018810148682314376)
XLA Ops:
  0.0 17.3 %contact.1 = f32[3,3072]{1,0:T(4,128)S(1)} custom-call(f32[24,12288]{1,0:T(8,128)} %node_any.1, s32[1,512]{1,0:T(1,128)} %bitcast.5, s32[1,12288]{1,0:T(1,128)} %bitcast.3, f32[3,8,128]{2,1,0:T(8,128)} %bitcast.4, f32[8,2,128]{2,1,0:T(2,128)} %sangle_any.1), custom_call_target="tpu_custom_call" | custom-call | tf_op jit(solution)/shard_map/contact/pallas_call | solution.py:417
  17.3 0.6 %copy.7 = f32[3,3072]{1,0:T(4,128)} copy(f32[3,3072]{1,0:T(4,128)S(1)} %contact.1) | data formatting | bytes 73728

commit v4 on v3

--- a/solution.py
+++ b/solution.py
@@ -233,8 +233,7 @@
     pltpu.make_async_copy(held(me), held(me), in_sem.at[0]).wait()
     pl.semaphore_wait(barrier, n_elem - 1 + jnp.where(leads, n_buck - 1, 0))
 
-    for u in range(n_elem - 1):
-        seg_copy(me, other(me, u)).start()
+    seg_copy(me, other(me, 0)).start()
 
     @pl.when(leads)
     def _():
@@ -255,6 +254,8 @@
 
     for u in range(n_elem - 1):
         cnt_copy(me, other(me, u)).start()
+    for u in range(1, n_elem - 1):
+        seg_copy(me, other(me, u)).start()
 
     @pl.when(jnp.logical_not(leads))
     def _():

time: 18.1 us -> 17.5 us (0.967)
  Pallas kernels: 17.3 us -> 16.8 us
    pallas_call x1, Pallas kernels: 17.3 us -> 16.8 us  [local(): pl.pallas_call(functools.partial(kernel, n_elem, n_buck), out_shape=jax.S...]
where the time goes in v4:
time: 17.5 us; the launch traced here: 17.4 us
  Pallas kernels  16.8 us (96%)
  local copies, waits for them, and re-layouts  0.62 us (4%)
    pallas_call x1, Pallas kernels, local(): pl.pallas_call(functools.partial(kernel, n_elem, n_buck), out_shape=jax.S...  16.8 us
    unnamed x1, local copies, waits for them, and re-layouts  0.62 us

profile of v4, /device:TPU:0, one launch (start us, length us, event | category | flops | bytes accessed | tf_op | source)
XLA Modules:
  0.0 17.4 jit_solution(5188222340713271805)
XLA Ops:
  0.0 16.8 %contact.1 = f32[3,3072]{1,0:T(4,128)S(1)} custom-call(f32[24,12288]{1,0:T(8,128)} %node_any.1, s32[1,512]{1,0:T(1,128)} %bitcast.5, s32[1,12288]{1,0:T(1,128)} %bitcast.3, f32[3,8,128]{2,1,0:T(8,128)} %bitcast.4, f32[8,2,128]{2,1,0:T(2,128)} %sangle_any.1), custom_call_target="tpu_custom_call" | custom-call | tf_op jit(solution)/shard_map/contact/pallas_call | solution.py:418
  16.8 0.6 %copy.7 = f32[3,3072]{1,0:T(4,128)} copy(f32[3,3072]{1,0:T(4,128)S(1)} %contact.1) | data formatting | bytes 73728
